TPU v7x, 32 devices: a whole 2x2x4 slice. The times are simulated.
32 devices in a mesh: dp: 4 (over y, core), expert: 4 (over z), tensor: 2 (over x).
Axes of the slice: x: 2, y: 2, z: 4, core: 2. Of those that a mesh axis runs over, the one named last changes fastest.
Arguments:
- router_input: bfloat16 [1024, 2048], P(('dp', 'expert'), 'tensor'), may hold values from -6 to 6
- router_weight: bfloat16 [2048, 8], replicated, may hold values from -0.125 to 0.125
- expert_ids: int32 [1024, 2], P(('dp', 'expert', 'tensor')), may hold values from 0 to 7, all different within a row; in each aligned block of 32 rows (0 to 31, 32 to 63, ...) at most 9 rows name the same one
- down_weight: bfloat16 [61440, 2048], P(('expert', 'tensor')), may hold values from -0.0625 to 0.0625
- hidden: bfloat16 [4, 72, 61440], P('dp', None, ('expert', 'tensor')), may hold values from -6 to 6
- grad_output: bfloat16 [1024, 2048], P(('dp', 'expert', 'tensor')), may hold values from -4 to 4
Outputs:
- weight_grad: bfloat16 [61440, 2048], P(('expert', 'tensor', 'dp'))
- hidden_grad: bfloat16 [4, 72, 61440], P('dp', None, ('expert', 'tensor'))
- router_grad: float32 [2048, 8], replicated
- input_grad: bfloat16 [1024, 2048], P(('dp', 'expert', 'tensor'))
Inputs may be any that keep to these rules, and one draw needn't show every extreme that they name: `expert_ids`: each row names 2 different experts. Within the 32 rows of one device no expert is named more than 9 times, and some device's rows name some expert exactly 9 times.
All inputs are finite; a program needn't handle non-finite values.
Results may differ from a plain program's by a relative error of at most 0.018.
Values may be sent and summed in bfloat16 or wider, within the bound.
No kernel may reach another device: no remote copies, remote signals or barrier semaphores. Data moves between devices by JAX's collectives and lax.ppermute only.
A program may use at most 192 MiB of HBM per device.

v0:
```python
import jax
import jax.numpy as jnp
from jax import lax
from jax.sharding import PartitionSpec as P


def per_device(router_input, router_weight, expert_ids, down_weight, hidden, grad_output):
    token_rows = grad_output.shape[0]
    model_width = grad_output.shape[1]
    expert_count = router_weight.shape[1]
    choose_count = expert_ids.shape[1]
    expert_ranks = lax.axis_size("expert")
    tensor_ranks = lax.axis_size("tensor")
    sources = expert_ranks * tensor_ranks
    spread = sources // expert_count
    capacity = hidden.shape[1] // sources
    full_input = lax.all_to_all(router_input, "tensor", split_axis=0, concat_axis=1, tiled=True)
    logits = jnp.dot(full_input, router_weight, preferred_element_type=jnp.float32)
    labels = jnp.arange(expert_count, dtype=jnp.int32)
    onehot_int = (expert_ids[:, :, None] == labels).astype(jnp.int32)
    onehot = onehot_int.astype(jnp.float32)
    picked = jnp.sum(onehot * logits[:, None, :], axis=2)
    first_gate = jax.nn.sigmoid(picked[:, 0] - picked[:, 1])
    second_gate = jax.nn.sigmoid(picked[:, 1] - picked[:, 0])
    gate_values = jnp.stack([first_gate, second_gate], axis=1)
    gate_low = gate_values.astype(jnp.bfloat16)
    flat_hits = onehot_int.reshape(token_rows * choose_count, expert_count)
    before = jnp.cumsum(flat_hits, axis=0) - flat_hits
    slot_pos = jnp.sum(before * flat_hits, axis=1).reshape(token_rows, choose_count)
    slot_ids = jnp.arange(capacity, dtype=jnp.int32)
    dispatch_table = onehot[:, :, :, None] * (slot_pos[:, :, None, None] == slot_ids).astype(
        jnp.float32
    )
    slot_table = jnp.sum(dispatch_table, axis=1).astype(jnp.bfloat16)
    packed_grad = jnp.einsum(
        "rec,rd->ecd", slot_table, grad_output, preferred_element_type=jnp.float32
    ).astype(jnp.bfloat16)
    packed_gate = jnp.einsum("rkec,rk->ec", dispatch_table, gate_low.astype(jnp.float32)).astype(
        jnp.bfloat16
    )
    send_grad = jnp.repeat(packed_grad, spread, axis=0)
    send_gate = jnp.repeat(packed_gate, spread, axis=0)
    recv_grad, recv_gate = (
        lax.all_to_all(send_grad, ("expert", "tensor"), split_axis=0, concat_axis=0, tiled=True),
        lax.all_to_all(send_gate, ("expert", "tensor"), split_axis=0, concat_axis=0, tiled=True),
    )
    recv_grad = recv_grad.reshape(sources * capacity, model_width)
    recv_gate = recv_gate.reshape(sources * capacity).astype(jnp.float32)
    hidden_rows = hidden[0]
    gated_grad = (recv_gate[:, None] * recv_grad.astype(jnp.float32)).astype(jnp.bfloat16)
    expert_image = lax.dot_general(
        recv_grad, down_weight, (((1,), (1,)), ((), ())), preferred_element_type=jnp.float32
    )
    hidden_part = (recv_gate[:, None] * expert_image).astype(jnp.bfloat16)
    gate_partial = jnp.sum(hidden_rows.astype(jnp.float32) * expert_image, axis=1).reshape(
        sources, capacity
    )
    returned = lax.all_to_all(
        gate_partial, ("expert", "tensor"), split_axis=0, concat_axis=0, tiled=True
    )
    expert_sums = jnp.sum(returned.reshape(expert_count, spread, capacity), axis=1)
    gate_grad = jnp.einsum("rkec,ec->rk", dispatch_table, expert_sums)
    mixed_term = jnp.sum(gate_values * gate_grad, axis=1, keepdims=True)
    logit_part = gate_values * (gate_grad - mixed_term)
    logit_grad = jnp.sum(onehot * logit_part[:, :, None], axis=1)
    input_grad = jnp.dot(
        logit_grad, router_weight.astype(jnp.float32).T, precision=lax.Precision.HIGHEST
    ).astype(jnp.bfloat16)
    router_local = jnp.dot(
        full_input.astype(jnp.float32).T, logit_grad, precision=lax.Precision.HIGHEST
    )
    router_grad = lax.psum(router_local, ("dp", "expert", "tensor"))
    weight_sum = lax.psum_scatter(
        lax.dot_general(
            hidden_rows, gated_grad, (((0,), (0,)), ((), ())), preferred_element_type=jnp.float32
        ).astype(jnp.bfloat16),
        "dp",
        scatter_dimension=0,
        tiled=True,
    )
    return (weight_sum, hidden_part[None], router_grad, input_grad)


def solution(mesh):
    return jax.shard_map(
        per_device,
        mesh=mesh,
        in_specs=(
            P(("dp", "expert"), "tensor"),
            P(),
            P(("dp", "expert", "tensor"), None),
            P(("expert", "tensor"), None),
            P("dp", None, ("expert", "tensor")),
            P(("dp", "expert", "tensor"), None),
        ),
        out_specs=(
            P(("expert", "tensor", "dp"), None),
            P("dp", None, ("expert", "tensor")),
            P(),
            P(("dp", "expert", "tensor"), None),
        ),
        check_vma=False,
    )
```

profile of v0, /device:TPU:0, one launch (start us, length us, event | category | flops | bytes accessed | tf_op | source)
XLA Modules:
  0.0 359.2 jit_solution(10456292851233868904)
XLA Ops:
  8.0 0.0 copy-start
  8.0 0.0 copy-start.2
  8.0 4.4 %all-to-all-start = ((bf16[2,32,1024]{2,1,0:T(8,128)(2,1)}), bf16[2,32,1024]{2,1,0:T(8,128)(2,1)S(1)}, u32[]{:S(2)}, u32[]{:S(2)}) async-start(bf16[2,32,1024]{2,1,0:T(8,128)(2,1)} %bitcast.52), calls=%async_computation | async-start | bytes 262144 | tf_op jit(solution)/shard_map/all_to_all | solution.py:17
  12.4 0.8 copy.28
  13.2 0.7 convert_convert_fusion
  13.8 0.1 eq.49
  13.9 0.1 fusion.10
  14.0 0.1 reduce_window_sum.11
  14.1 0.2 select_reduce_fusion
  14.3 0.1 eq.53
  14.4 0.1 copy.29
  14.5 2.4 all-to-all-done
  17.0 0.9 fusion.15
  17.9 0.7 multiply_reduce_fusion.3
  18.6 0.2 fusion.2
  18.8 0.1 copy.37
  18.9 0.6 copy.31
  19.5 5.4 %all-to-all-start.1 = ((bf16[8,1,9]{2,1,0:T(2,128)(2,1)}), bf16[8,1,9]{2,1,0:T(2,128)(2,1)S(1)}, u32[]{:S(2)}, u32[]{:S(2)}) async-start(bf16[8,1,9]{2,1,0:T(2,128)(2,1)} %copy.31), calls=%async_computation.1 | async-start | bytes 8192 | tf_op jit(solution)/shard_map/all_to_all | solution.py:45
  24.9 0.0 copy-done
  24.9 1.1 convolution_convert_fusion
  26.0 5.3 %all-to-all-done.1 = bf16[8,1,9]{2,1,0:T(2,128)(2,1)S(1)} async-done(((bf16[8,1,9]{2,1,0:T(2,128)(2,1)}), bf16[8,1,9]{2,1,0:T(2,128)(2,1)S(1)}, u32[]{:S(2)}, u32[]{:S(2)}) %all-to-all-start.1) | async-done | bytes 176 | tf_op jit(solution)/shard_map/all_to_all | solution.py:45
  31.3 3.5 all-to-all-start.2
  34.9 0.1 reshape.65
  34.9 12.0 %all-to-all-done.2 = bf16[8,9,2048]{2,1,0:T(8,128)(2,1)S(1)} async-done(((bf16[8,9,2048]{2,1,0:T(8,128)(2,1)}), bf16[8,9,2048]{2,1,0:T(8,128)(2,1)S(1)}, u32[]{:S(2)}, u32[]{:S(2)}) %all-to-all-start.2) | async-done | bytes 294944 | tf_op jit(solution)/shard_map/all_to_all | solution.py:44
  47.0 0.1 reshape.63
  47.1 0.0 copy-done.2
  47.1 0.0 copy-start.4
  47.1 15.5 %multiply_reduce_fusion = (f32[72]{0:T(128)S(1)}, bf16[1,72,7680]{2,1,0:T(8,128)(2,1)}) fusion(bf16[1,72,7680]{2,1,0:T(8,128)(2,1)S(1)} %copy-done.2, f32[72]{0:T(128)S(1)} %reshape.65, bf16[72,2048]{1,0:T(8,128)(2,1)S(1)} %reshape.63, bf16[7680,2048]{1,0:T(8,128)(2,1)} %param.9), kind=kOutput, calls=%fused_computation.4 | convolution fusion | flops 2267688960 | bytes 33964608 | tf_op jit(solution)/shard_map/dot_general | solution.py:51
  62.6 0.7 all_to_all.36
  63.3 3.7 %all-to-all-start.3 = ((f32[8,1,9]{2,1,0:T(1,128)}), f32[8,1,9]{2,1,0:T(1,128)S(1)}, u32[]{:S(2)}, u32[]{:S(2)}) async-start(f32[8,1,9]{2,1,0:T(1,128)} %bitcast.12), calls=%async_computation.3 | async-start | bytes 8192 | tf_op jit(solution)/shard_map/all_to_all | solution.py:58
  67.0 0.0 all-reduce.2.cloned.1.call-start
  67.0 0.2 multiply_convert_fusion.1
  67.2 0.1 convert_element_type.93
  67.3 6.1 %all-to-all-done.3 = f32[8,1,9]{2,1,0:T(1,128)S(1)} async-done(((f32[8,1,9]{2,1,0:T(1,128)}), f32[8,1,9]{2,1,0:T(1,128)S(1)}, u32[]{:S(2)}, u32[]{:S(2)}) %all-to-all-start.3) | async-done | bytes 320 | tf_op jit(solution)/shard_map/all_to_all | solution.py:58
  73.4 0.1 copy.45
  73.5 0.1 fusion.6
  73.6 0.0 copy-done.4
  73.6 0.8 convolution_bitcast_fusion
  74.4 0.0 all-reduce.2.cloned.1.call-update
  74.5 0.0 reduce-scatter.4.cloned.1.call-start
  74.5 13.9 %convert_bitcast_fusion = bf16[7680,2048]{0,1:T(8,128)(2,1)} fusion(bf16[72,2048]{1,0:T(8,128)(2,1)S(1)} %convert_element_type.93, bf16[1,72,7680]{2,1,0:T(8,128)(2,1)S(1)} %copy-done.2), kind=kOutput, calls=%fused_computation | convolution fusion | flops 2280652800 | bytes 32858112 | tf_op jit(solution)/shard_map/dot_general | solution.py:74
  88.4 40.7 %copy.43 = bf16[7680,2048]{1,0:T(8,128)(2,1)} copy(bf16[7680,2048]{0,1:T(8,128)(2,1)} %convert_bitcast_fusion) | data formatting | bytes 62914560
  129.0 0.0 copy-start.3
  129.0 0.0 reduce-scatter.4.cloned.1.call-update
  129.1 0.7 copy-done.3
  129.8 0.0 copy-start.1
  129.8 1.0 convolution_convert_fusion.1
  130.8 159.6 %all-reduce.2.cloned.1.call-done = f32[2048,8]{0,1:T(8,128)} async-done(((f32[2048,8]{0,1:T(8,128)}), f32[2048,8]{0,1:T(8,128)}) %all-reduce.2.cloned.1.call-update) | async-done | bytes 65552 | tf_op jit(solution)/shard_map/psum | solution.py:72
  290.4 59.9 %reduce-scatter.4.cloned.1.call-done = bf16[1920,2048]{1,0:T(8,128)(2,1)} async-done(((bf16[7680,2048]{1,0:T(8,128)(2,1)}), bf16[1920,2048]{1,0:T(8,128)(2,1)}) %reduce-scatter.4.cloned.1.call-update) | async-done | bytes 7864336
  350.2 1.5 copy.55
  351.7 0.0 copy-done.1
  (10 shorter events, 0.1 us)
Async XLA Ops:
  8.0 16.9 %copy-start = (bf16[32,2048]{1,0:T(8,128)(2,1)S(1)}, bf16[32,2048]{1,0:T(8,128)(2,1)}, u32[]{:S(2)}) copy-start(bf16[32,2048]{1,0:T(8,128)(2,1)} %param.11) | copy-start | bytes 393220
  8.0 39.1 %copy-start.2 = (bf16[1,72,7680]{2,1,0:T(8,128)(2,1)S(1)}, bf16[1,72,7680]{2,1,0:T(8,128)(2,1)}, u32[]{:S(2)}) copy-start(bf16[1,72,7680]{2,1,0:T(8,128)(2,1)} %param.10) | copy-start | bytes 3317764
  8.0 8.9 %all-to-all-start = ((bf16[2,32,1024]{2,1,0:T(8,128)(2,1)}), bf16[2,32,1024]{2,1,0:T(8,128)(2,1)S(1)}, u32[]{:S(2)}, u32[]{:S(2)}) async-start(bf16[2,32,1024]{2,1,0:T(8,128)(2,1)} %bitcast.52), calls=%async_computation | async-start | bytes 262144 | tf_op jit(solution)/shard_map/all_to_all | solution.py:17
  19.5 11.8 %all-to-all-start.1 = ((bf16[8,1,9]{2,1,0:T(2,128)(2,1)}), bf16[8,1,9]{2,1,0:T(2,128)(2,1)S(1)}, u32[]{:S(2)}, u32[]{:S(2)}) async-start(bf16[8,1,9]{2,1,0:T(2,128)(2,1)} %copy.31), calls=%async_computation.1 | async-start | bytes 8192 | tf_op jit(solution)/shard_map/all_to_all | solution.py:45
  31.3 15.6 %all-to-all-start.2 = ((bf16[8,9,2048]{2,1,0:T(8,128)(2,1)}), bf16[8,9,2048]{2,1,0:T(8,128)(2,1)S(1)}, u32[]{:S(2)}, u32[]{:S(2)}) async-start(bf16[8,9,2048]{2,1,0:T(8,128)(2,1)} %convolution_convert_fusion), calls=%async_computation.2 | async-start | bytes 1048576 | tf_op jit(solution)/shard_map/all_to_all | solution.py:44
  47.1 26.5 %copy-start.4 = (s32[32,2]{0,1:T(2,128)S(1)}, s32[32,2]{0,1:T(2,128)}, u32[]{:S(2)}) copy-start(s32[32,2]{0,1:T(2,128)} %param.8) | copy-start | bytes 772
  63.3 10.1 %all-to-all-start.3 = ((f32[8,1,9]{2,1,0:T(1,128)}), f32[8,1,9]{2,1,0:T(1,128)S(1)}, u32[]{:S(2)}, u32[]{:S(2)}) async-start(f32[8,1,9]{2,1,0:T(1,128)} %bitcast.12), calls=%async_computation.3 | async-start | bytes 8192 | tf_op jit(solution)/shard_map/all_to_all | solution.py:58
  67.0 223.4 %all-reduce.2.cloned.1.call-start = ((), (), s32[]{:S(2)}) async-start(), calls=%async_computation.5 | async-start | bytes 131072 | tf_op jit(solution)/shard_map/psum | solution.py:72
  74.5 275.8 %reduce-scatter.4.cloned.1.call-start = ((), (), s32[]{:S(2)}) async-start(), calls=%async_computation.6 | async-start | bytes 39321600
  129.0 0.8 copy-start.3
  129.8 221.9 %copy-start.1 = (bf16[32,2048]{1,0:T(8,128)(2,1)S(1)}, bf16[32,2048]{1,0:T(8,128)(2,1)}, u32[]{:S(2)}) copy-start(bf16[32,2048]{1,0:T(8,128)(2,1)} %param.11) | copy-start | bytes 393220
Sparse Core Ops, SparseCore 0:
  74.6 215.7 all-reduce.1
Sparse Core Ops, SparseCore 1:
  129.2 221.0 reduce-scatter.3
where the time goes:
time: 361 us; the launch traced here: 359 us
  waiting for transfers between devices  245 us (68%)
  local copies, waits for them, and re-layouts  45.8 us (13%)
  matrix products  33.3 us (9%)
  starting transfers between devices  17 us (5%)
  between operations  15.6 us (4%)
    psum x1, waiting for transfers between devices, per_device(): router_grad = lax.psum(router_local, ('dp', 'expert', 'tensor'))  160 us
    unnamed x3, waiting for transfers between devices  59.9 us
    unnamed x14, local copies, waits for them, and re-layouts  43.7 us
    dot_general x1, matrix products, per_device(): lax.dot_general(recv_grad, down_weight, (((1,), (1,)), ((), ())), preferr...  15.5 us
    dot_general x1, matrix products, per_device(): lax.dot_general(hidden_rows, gated_grad, (((0,), (0,)), ((), ())), prefer...  13.9 us
    all_to_all x1, waiting for transfers between devices, per_device(): lax.all_to_all(send_grad, ('expert', 'tensor'), split_axis=0, concat_axis...  12 us
  transfers between devices with their start and end apart: 6, of which 6 were waited for; matrix products, arithmetic and copies ran while one was open for 16% of the time, Pallas kernels for 0%

commit v1 on v0

--- a/solution.py
+++ b/solution.py
@@ -69,7 +69,7 @@
     router_local = jnp.dot(
         full_input.astype(jnp.float32).T, logit_grad, precision=lax.Precision.HIGHEST
     )
-    router_grad = lax.psum(router_local, ("dp", "expert", "tensor"))
+    router_grad = lax.psum(lax.psum(router_local, ("expert", "tensor")), "dp")
     weight_sum = lax.psum_scatter(
         lax.dot_general(
             hidden_rows, gated_grad, (((0,), (0,)), ((), ())), preferred_element_type=jnp.float32

time: 361 us -> 428 us (1.19)
  waiting for transfers between devices: 245 us -> 308 us
  blocking collectives: 0 us -> 9.96 us
    unnamed x3 -> x4, waiting for transfers between devices: 59.9 us -> 222 us
    psum x1 -> x2, waiting for transfers between devices: 160 us -> 66.4 us  [per_device(): router_grad = lax.psum(lax.psum(router_local, ('expert', 'tensor')), 'dp')]
    all_to_all x0 -> x1, blocking collectives: none -> 9.96 us  [per_device(): lax.all_to_all(gate_partial, ('expert', 'tensor'), split_axis=0, concat_a...]
    all_to_all x1 -> x0, waiting for transfers between devices: 6.07 us -> none  [per_device(): lax.all_to_all(gate_partial, ('expert', 'tensor'), split_axis=0, concat_a...]
  transfers between devices with their start and end apart: 6 -> 6, of which waited for: 6 -> 5; matrix products, arithmetic and copies ran while one was open for 16% -> 14% of each run, Pallas kernels for 0% -> 0%
where the time goes in v1:
time: 428 us; the launch traced here: 426 us
  waiting for transfers between devices  308 us (72%)
  local copies, waits for them, and re-layouts  45.2 us (11%)
  matrix products  33.2 us (8%)
  between operations  13.9 us (3%)
  starting transfers between devices  13.4 us (3%)
  blocking collectives  9.96 us (2%)
    unnamed x4, waiting for transfers between devices  222 us
    psum x2, waiting for transfers between devices, per_device(): router_grad = lax.psum(lax.psum(router_local, ('expert', 'tensor')), 'dp')  66.4 us
    unnamed x14, local copies, waits for them, and re-layouts  43.8 us
    dot_general x1, matrix products, per_device(): lax.dot_general(recv_grad, down_weight, (((1,), (1,)), ((), ())), preferr...  15.5 us
    dot_general x1, matrix products, per_device(): lax.dot_general(hidden_rows, gated_grad, (((0,), (0,)), ((), ())), prefer...  13.8 us
    all_to_all x1, waiting for transfers between devices, per_device(): lax.all_to_all(send_grad, ('expert', 'tensor'), split_axis=0, concat_axis...  12 us
    all_to_all x1, blocking collectives, per_device(): lax.all_to_all(gate_partial, ('expert', 'tensor'), split_axis=0, concat_a...  9.96 us
  transfers between devices with their start and end apart: 6, of which 5 were waited for; matrix products, arithmetic and copies ran while one was open for 14% of the time, Pallas kernels for 0%

profile of v1, /device:TPU:0, one launch (start us, length us, event | category | flops | bytes accessed | tf_op | source)
XLA Modules:
  0.0 426.0 jit_solution(9705284663293806943)
XLA Ops:
  7.2 0.0 copy-start
  7.2 0.0 copy-start.2
  7.2 4.4 %all-to-all-start = ((bf16[2,32,1024]{2,1,0:T(8,128)(2,1)}), bf16[2,32,1024]{2,1,0:T(8,128)(2,1)S(1)}, u32[]{:S(2)}, u32[]{:S(2)}) async-start(bf16[2,32,1024]{2,1,0:T(8,128)(2,1)} %bitcast.52), calls=%async_computation | async-start | bytes 262144 | tf_op jit(solution)/shard_map/all_to_all | solution.py:17
  11.6 0.8 copy.28
  12.3 0.7 convert_convert_fusion
  13.0 0.1 eq.49
  13.1 0.1 fusion.10
  13.2 0.1 reduce_window_sum.11
  13.3 0.2 select_reduce_fusion
  13.5 0.1 eq.53
  13.6 0.1 copy.29
  13.7 2.4 all-to-all-done
  16.1 0.9 fusion.15
  17.0 0.7 multiply_reduce_fusion.3
  17.8 0.2 fusion.2
  18.0 0.1 copy.37
  18.1 0.6 copy.31
  18.7 5.4 %all-to-all-start.1 = ((bf16[8,1,9]{2,1,0:T(2,128)(2,1)}), bf16[8,1,9]{2,1,0:T(2,128)(2,1)S(1)}, u32[]{:S(2)}, u32[]{:S(2)}) async-start(bf16[8,1,9]{2,1,0:T(2,128)(2,1)} %copy.31), calls=%async_computation.1 | async-start | bytes 8192 | tf_op jit(solution)/shard_map/all_to_all | solution.py:45
  24.1 0.0 copy-done
  24.1 1.1 convolution_convert_fusion
  25.2 5.3 %all-to-all-done.1 = bf16[8,1,9]{2,1,0:T(2,128)(2,1)S(1)} async-done(((bf16[8,1,9]{2,1,0:T(2,128)(2,1)}), bf16[8,1,9]{2,1,0:T(2,128)(2,1)S(1)}, u32[]{:S(2)}, u32[]{:S(2)}) %all-to-all-start.1) | async-done | bytes 176 | tf_op jit(solution)/shard_map/all_to_all | solution.py:45
  30.5 3.5 all-to-all-start.2
  34.0 0.0 all-reduce.3.cloned.1.call-start
  34.1 0.1 reshape.65
  34.1 12.0 %all-to-all-done.2 = bf16[8,9,2048]{2,1,0:T(8,128)(2,1)S(1)} async-done(((bf16[8,9,2048]{2,1,0:T(8,128)(2,1)}), bf16[8,9,2048]{2,1,0:T(8,128)(2,1)S(1)}, u32[]{:S(2)}, u32[]{:S(2)}) %all-to-all-start.2) | async-done | bytes 294944 | tf_op jit(solution)/shard_map/all_to_all | solution.py:44
  46.1 0.1 reshape.63
  46.3 0.0 copy-done.2
  46.3 0.0 copy-start.4
  46.3 15.5 %multiply_reduce_fusion = (f32[72]{0:T(128)S(1)}, bf16[1,72,7680]{2,1,0:T(8,128)(2,1)}) fusion(bf16[1,72,7680]{2,1,0:T(8,128)(2,1)S(1)} %copy-done.2, f32[72]{0:T(128)S(1)} %reshape.65, bf16[72,2048]{1,0:T(8,128)(2,1)S(1)} %reshape.63, bf16[7680,2048]{1,0:T(8,128)(2,1)} %param.9), kind=kOutput, calls=%fused_computation.4 | convolution fusion | flops 2267688960 | bytes 33964608 | tf_op jit(solution)/shard_map/dot_general | solution.py:51
  61.8 0.1 all_to_all.36
  61.9 10.0 %all_to_all.42 = f32[8,1,9]{2,1,0:T(1,128)S(1)} all-to-all(f32[8,1,9]{2,1,0:T(1,128)S(1)} %bitcast.54), channel_id=1, replica_groups=mesh['dp'=4,'expert'=4,'tensor'=2] {'expert','tensor'}, dimensions={0} | all-to-all | bytes 576 | tf_op jit(solution)/shard_map/all_to_all | solution.py:58
  71.8 0.1 copy.45
  71.9 0.1 fusion.6
  72.0 0.0 copy-done.4
  72.1 0.8 convolution_bitcast_fusion
  72.9 0.0 all-reduce.3.cloned.1.call-update
  72.9 0.0 all-reduce.5.cloned.1.call-start
  72.9 0.2 multiply_convert_fusion.1
  73.1 0.1 convert_element_type.93
  73.2 66.4 %all-reduce.3.cloned.1.call-done = f32[2048,8]{0,1:T(8,128)} async-done(((f32[2048,8]{0,1:T(8,128)}), f32[2048,8]{0,1:T(8,128)}) %all-reduce.3.cloned.1.call-update) | async-done | bytes 65552 | tf_op jit(solution)/shard_map/psum | solution.py:72
  139.6 0.0 all-reduce.5.cloned.1.call-update
  139.6 0.0 reduce-scatter.4.cloned.1.call-start
  139.7 13.8 %convert_bitcast_fusion = bf16[7680,2048]{0,1:T(8,128)(2,1)} fusion(bf16[72,2048]{1,0:T(8,128)(2,1)S(1)} %convert_element_type.93, bf16[1,72,7680]{2,1,0:T(8,128)(2,1)S(1)} %copy-done.2), kind=kOutput, calls=%fused_computation | convolution fusion | flops 2280652800 | bytes 32858112 | tf_op jit(solution)/shard_map/dot_general | solution.py:74
  153.4 40.7 %copy.43 = bf16[7680,2048]{1,0:T(8,128)(2,1)} copy(bf16[7680,2048]{0,1:T(8,128)(2,1)} %convert_bitcast_fusion) | data formatting | bytes 62914560
  194.2 0.0 copy-start.3
  194.2 0.0 reduce-scatter.4.cloned.1.call-update
  194.2 0.7 copy-done.3
  194.9 0.0 copy-start.1
  194.9 1.0 convolution_convert_fusion.1
  195.9 0.0 all-reduce.5.cloned.1.call-done
  195.9 222.1 %reduce-scatter.4.cloned.1.call-done = bf16[1920,2048]{1,0:T(8,128)(2,1)} async-done(((bf16[7680,2048]{1,0:T(8,128)(2,1)}), bf16[1920,2048]{1,0:T(8,128)(2,1)}) %reduce-scatter.4.cloned.1.call-update) | async-done | bytes 7864336
  418.0 1.5 copy.56
  419.4 0.0 copy-done.1
  (10 shorter events, 0.1 us)
Async XLA Ops:
  7.2 16.9 %copy-start = (bf16[32,2048]{1,0:T(8,128)(2,1)S(1)}, bf16[32,2048]{1,0:T(8,128)(2,1)}, u32[]{:S(2)}) copy-start(bf16[32,2048]{1,0:T(8,128)(2,1)} %param.11) | copy-start | bytes 393220
  7.2 39.1 %copy-start.2 = (bf16[1,72,7680]{2,1,0:T(8,128)(2,1)S(1)}, bf16[1,72,7680]{2,1,0:T(8,128)(2,1)}, u32[]{:S(2)}) copy-start(bf16[1,72,7680]{2,1,0:T(8,128)(2,1)} %param.10) | copy-start | bytes 3317764
  7.2 8.9 %all-to-all-start = ((bf16[2,32,1024]{2,1,0:T(8,128)(2,1)}), bf16[2,32,1024]{2,1,0:T(8,128)(2,1)S(1)}, u32[]{:S(2)}, u32[]{:S(2)}) async-start(bf16[2,32,1024]{2,1,0:T(8,128)(2,1)} %bitcast.52), calls=%async_computation | async-start | bytes 262144 | tf_op jit(solution)/shard_map/all_to_all | solution.py:17
  18.7 11.8 %all-to-all-start.1 = ((bf16[8,1,9]{2,1,0:T(2,128)(2,1)}), bf16[8,1,9]{2,1,0:T(2,128)(2,1)S(1)}, u32[]{:S(2)}, u32[]{:S(2)}) async-start(bf16[8,1,9]{2,1,0:T(2,128)(2,1)} %copy.31), calls=%async_computation.1 | async-start | bytes 8192 | tf_op jit(solution)/shard_map/all_to_all | solution.py:45
  30.5 15.6 %all-to-all-start.2 = ((bf16[8,9,2048]{2,1,0:T(8,128)(2,1)}), bf16[8,9,2048]{2,1,0:T(8,128)(2,1)S(1)}, u32[]{:S(2)}, u32[]{:S(2)}) async-start(bf16[8,9,2048]{2,1,0:T(8,128)(2,1)} %convolution_convert_fusion), calls=%async_computation.2 | async-start | bytes 1048576 | tf_op jit(solution)/shard_map/all_to_all | solution.py:44
  34.0 105.6 %all-reduce.3.cloned.1.call-start = ((), (), s32[]{:S(2)}) async-start(), calls=%async_computation.5 | async-start | bytes 131072 | tf_op jit(solution)/shard_map/psum | solution.py:72
  46.3 25.8 %copy-start.4 = (s32[32,2]{0,1:T(2,128)S(1)}, s32[32,2]{0,1:T(2,128)}, u32[]{:S(2)}) copy-start(s32[32,2]{0,1:T(2,128)} %param.8) | copy-start | bytes 772
  72.9 123.0 %all-reduce.5.cloned.1.call-start = ((), (), s32[]{:S(2)}) async-start(), calls=%async_computation.6 | async-start | bytes 131072 | tf_op jit(solution)/shard_map/psum | solution.py:72
  139.6 278.3 %reduce-scatter.4.cloned.1.call-start = ((), (), s32[]{:S(2)}) async-start(), calls=%async_computation.7 | async-start | bytes 39321600
  194.2 0.8 copy-start.3
  194.9 224.5 %copy-start.1 = (bf16[32,2048]{1,0:T(8,128)(2,1)S(1)}, bf16[32,2048]{1,0:T(8,128)(2,1)}, u32[]{:S(2)}) copy-start(bf16[32,2048]{1,0:T(8,128)(2,1)} %param.11) | copy-start | bytes 393220
Sparse Core Ops, SparseCore 0:
  73.0 66.5 all-reduce.2
  141.9 31.4 all-reduce.4
  194.3 223.5 reduce-scatter.3
